TPU v7x, 32 devices: a whole 2x2x4 slice. The times are simulated.
32 devices in a mesh: parts: 2 (over y), expert: 4 (over z), tensor: 4 (over x, core).
Axes of the slice: x: 2, y: 2, z: 4, core: 2. Of those that a mesh axis runs over, the one named last changes fastest.
Arguments:
- mamba_input: bfloat16 [128, 4096], P(('parts', 'expert'), 'tensor'), parts along dimension 0, may hold values from -5 to 5
- mamba_gate: bfloat16 [128, 4096], P(('parts', 'expert'), 'tensor'), parts along dimension 0, may hold values from -5 to 5
- conv_state: bfloat16 [128, 3, 4096], P(('parts', 'expert'), None, 'tensor'), parts along dimension 0, may hold values from -5 to 5
- scan_state: float32 [128, 16, 4096], P(('parts', 'expert'), None, 'tensor'), parts along dimension 0, may hold values from -6 to 6
- conv_weight: float32 [4, 4096], P(None, 'tensor'), may hold values from -3 to 3
- conv_bias: float32 [4096], P('tensor'), may hold values from -0.5 to 0.5
- state_proj: bfloat16 [288, 4096], P(None, 'tensor'), may hold values from -0.09375 to 0.09375
- step_proj: bfloat16 [256, 4096], P(None, 'tensor'), may hold values from -0.375 to 0.375
- step_bias: float32 [4096], P('tensor'), may hold values from -4.5 to -1
- decay_log: float32 [16, 4096], P(None, 'tensor'), may hold values from 0 to 2.8
- skip_gain: float32 [4096], P('tensor'), may hold values from 0.5 to 2
- queries: bfloat16 [128, 32, 128], P(('parts', 'expert'), 'tensor'), parts along dimension 0, may hold values from -48 to 48
- new_entry: bfloat16 [128, 8, 256], P(('parts', 'expert'), 'tensor'), parts along dimension 0, may hold values from -4 to 4
- past_entries: bfloat16 [128, 8, 128, 256], P(('parts', 'expert'), 'tensor'), parts along dimension 0, may hold values from -4 to 4
- lengths: int32 [128], P(('parts', 'expert')), parts along dimension 0, may hold values from 2 to 128, as said below
- expert_input: bfloat16 [128, 2048], P(('parts', 'expert'), 'tensor'), parts along dimension 0, may hold values from -5 to 5
- routes: int32 [128, 2], P(('parts', 'expert')), parts along dimension 0, may hold values from 0 to 7, as said below
- slots: int32 [128, 2], P(('parts', 'expert')), parts along dimension 0, may hold values from 0 to 7, as said below
- gates: float32 [128, 2], P(('parts', 'expert')), parts along dimension 0, may hold values from 0.1 to 1
- inner_weights: bfloat16 [8, 2, 8192, 2048], P('expert', None, 'tensor'), may hold values from -0.125 to 0.125
- outer_weights: bfloat16 [8, 8192, 2048], P('expert', 'tensor'), may hold values from -0.09375 to 0.09375
Outputs:
- mamba_out: bfloat16 [128, 4096], P(('parts', 'expert'), 'tensor'), parts along dimension 0
- next_state: float32 [128, 16, 4096], P(('parts', 'expert'), None, 'tensor'), parts along dimension 0
- attention_out: bfloat16 [128, 4096], P(('parts', 'expert'), 'tensor'), parts along dimension 0
- expert_out: bfloat16 [128, 2048], P(('parts', 'expert'), 'tensor'), parts along dimension 0
There are 2 independent parts, one for each index of `parts`. A program takes and returns all parts, laid end to end along the dimension named above; an argument that names none is the same for every part. Nothing has to cross between parts.
Inputs may be any that keep to these rules, and one draw needn't show every extreme that they name: `routes`: A row names 2 different experts. Within the 16 rows of one device (aligned blocks) no expert is named more than 8 times, and one expert, the same in all blocks, is named exactly 8 times in every block. slots[t, k] numbers the rows of t's block that name expert routes[t, k]: within a block the slots of one expert are distinct. `lengths`: every block of 16 sequences holds one of length 128.
All inputs are finite; a program needn't handle non-finite values.
Results may differ from a plain program's by a relative error of at most 0.006.
Values may be sent and summed in bfloat16 or wider, within the bound.
No kernel may reach another device: no remote copies, remote signals or barrier semaphores. Data moves between devices by JAX's collectives and lax.ppermute only.
A program may use at most 128 MiB of HBM per device.

v0:
```python
import jax
import jax.numpy as jnp
from jax import lax
from jax.sharding import PartitionSpec as P

EXPERTS = 8


def mamba_step(
    mamba_input,
    mamba_gate,
    conv_state,
    scan_state,
    conv_weight,
    conv_bias,
    state_proj,
    step_proj,
    step_bias,
    decay_log,
    skip_gain,
):
    window = jnp.concatenate(
        [conv_state.astype(jnp.float32), mamba_input.astype(jnp.float32)[:, None, :]], axis=1
    )
    conv_act = jax.nn.silu(jnp.sum(window * conv_weight[None], axis=1) + conv_bias)
    local_mix = lax.dot_general(
        conv_act.astype(jnp.bfloat16),
        state_proj,
        (((1,), (1,)), ((), ())),
        preferred_element_type=jnp.float32,
    )
    mixing = lax.psum(local_mix, "tensor")
    low_rank = step_proj.shape[0]
    states = decay_log.shape[0]
    step_size = jax.nn.softplus(
        jnp.dot(
            mixing[:, :low_rank].astype(jnp.bfloat16), step_proj, preferred_element_type=jnp.float32
        )
        + step_bias
    )
    in_coef = mixing[:, low_rank : low_rank + states]
    out_coef = mixing[:, low_rank + states :]
    decay_rate = jnp.exp(-step_size[:, None, :] * jnp.exp(decay_log)[None])
    next_state = decay_rate * scan_state + (step_size * conv_act)[:, None, :] * in_coef[:, :, None]
    mixed_out = jnp.sum(next_state * out_coef[:, :, None], axis=1) + skip_gain * conv_act
    return (
        (mixed_out * jax.nn.silu(mamba_gate.astype(jnp.float32))).astype(jnp.bfloat16),
        next_state,
    )


def attend(queries, new_entry, past_entries, lengths):
    seq_count, head_count, head_size = queries.shape
    groups = past_entries.shape[1]
    per_group = head_count // groups
    positions = past_entries.shape[2]
    scaling = head_size ** (-0.5)
    query_rows = queries.reshape(seq_count, groups, per_group, head_size)
    scores = (
        jnp.einsum(
            "sgqd,sgld->sgql",
            query_rows,
            past_entries[..., :head_size],
            preferred_element_type=jnp.float32,
        )
        * scaling
    )
    own_score = (
        jnp.einsum(
            "sgqd,sgd->sgq",
            query_rows,
            new_entry[..., :head_size],
            preferred_element_type=jnp.float32,
        )
        * scaling
    )
    live_mask = jnp.arange(positions, dtype=jnp.int32)[None, :] < lengths[:, None]
    scores = jnp.where(live_mask[:, None, None, :], scores, -jnp.inf)
    highest = jnp.maximum(jnp.max(scores, axis=3), own_score)
    weights = jnp.exp(scores - highest[..., None])
    own_weight = jnp.exp(own_score - highest)
    denominator = jnp.sum(weights, axis=3) + own_weight
    weights_low = (weights / denominator[..., None]).astype(jnp.bfloat16)
    own_low = (own_weight / denominator).astype(jnp.bfloat16)
    mixed_out = jnp.einsum(
        "sgql,sgld->sgqd",
        weights_low,
        past_entries[..., head_size:],
        preferred_element_type=jnp.float32,
    )
    mixed_out = (
        mixed_out
        + own_low.astype(jnp.float32)[..., None]
        * new_entry[..., head_size:].astype(jnp.float32)[:, :, None, :]
    )
    return mixed_out.reshape(seq_count, head_count * head_size).astype(jnp.bfloat16)


def shards(
    mamba_input,
    mamba_gate,
    conv_state,
    scan_state,
    conv_weight,
    conv_bias,
    state_proj,
    step_proj,
    step_bias,
    decay_log,
    skip_gain,
    queries,
    new_entry,
    past_entries,
    lengths,
    expert_input,
    routes,
    slots,
    gates,
    inner_weights,
    outer_weights,
):
    peer_count = lax.axis_size("expert")
    token_count = routes.shape[0]
    capacity = max(2, 4 * token_count // EXPERTS)
    replicas = max(1, peer_count // EXPERTS)
    local_rows = inner_weights.shape[0]
    total_rows = peer_count * local_rows
    row_expert = jnp.arange(total_rows, dtype=jnp.int32) // replicas
    slot_index = jnp.arange(capacity, dtype=jnp.int32)
    matches = (row_expert[:, None, None, None] == routes[None, None, :, :]) & (
        slot_index[None, :, None, None] == slots[None, None, :, :]
    )
    send_table = jnp.any(matches, axis=3).astype(jnp.bfloat16)
    weight_table = jnp.sum(jnp.where(matches, gates[None, None, :, :], 0.0), axis=3)
    features = lax.all_gather(expert_input, "tensor", axis=1, tiled=True)
    outgoing = jnp.einsum(
        "rcb,bd->rcd", send_table, features, preferred_element_type=jnp.float32
    ).astype(jnp.bfloat16)
    outgoing = outgoing.reshape(peer_count, local_rows, capacity, features.shape[1])
    gate_rows = inner_weights[:, 0]
    up_rows = inner_weights[:, 1]
    received = lax.all_to_all(outgoing, "expert", split_axis=0, concat_axis=0, tiled=True)
    gate_val = jnp.einsum("nlcd,lfd->nlcf", received, gate_rows, preferred_element_type=jnp.float32)
    up_val = jnp.einsum("nlcd,lfd->nlcf", received, up_rows, preferred_element_type=jnp.float32)
    hidden = (jax.nn.silu(gate_val) * up_val).astype(jnp.bfloat16)
    partial_value = jnp.einsum(
        "nlcf,lfd->nlcd", hidden, outer_weights, preferred_element_type=jnp.float32
    )
    share_sum = lax.psum_scatter(partial_value, "tensor", scatter_dimension=3, tiled=True)
    returned = lax.all_to_all(share_sum, "expert", split_axis=0, concat_axis=0, tiled=True)
    returned = returned.reshape(total_rows, capacity, returned.shape[3])
    merged = jnp.einsum("rcb,rcd->bd", weight_table, returned, precision=lax.Precision.HIGHEST)
    expert_out = merged.astype(jnp.bfloat16)
    mamba_out, next_state = mamba_step(
        mamba_input,
        mamba_gate,
        conv_state,
        scan_state,
        conv_weight,
        conv_bias,
        state_proj,
        step_proj,
        step_bias,
        decay_log,
        skip_gain,
    )
    attention_out = attend(queries, new_entry, past_entries, lengths)
    return (mamba_out, next_state, attention_out, expert_out)


def solution(mesh):
    return jax.shard_map(
        shards,
        mesh=mesh,
        in_specs=(
            P(("parts", "expert"), "tensor"),
            P(("parts", "expert"), "tensor"),
            P(("parts", "expert"), None, "tensor"),
            P(("parts", "expert"), None, "tensor"),
            P(None, "tensor"),
            P("tensor"),
            P(None, "tensor"),
            P(None, "tensor"),
            P("tensor"),
            P(None, "tensor"),
            P("tensor"),
            P(("parts", "expert"), "tensor", None),
            P(("parts", "expert"), "tensor", None),
            P(("parts", "expert"), "tensor", None, None),
            P(("parts", "expert")),
            P(("parts", "expert"), "tensor"),
            P(("parts", "expert"), None),
            P(("parts", "expert"), None),
            P(("parts", "expert"), None),
            P("expert", None, "tensor", None),
            P("expert", "tensor", None),
        ),
        out_specs=(
            P(("parts", "expert"), "tensor"),
            P(("parts", "expert"), None, "tensor"),
            P(("parts", "expert"), "tensor"),
            P(("parts", "expert"), "tensor"),
        ),
        check_vma=False,
    )
```

profile of v0, /device:TPU:0, one launch (start us, length us, event | category | flops | bytes accessed | tf_op | source)
XLA Modules:
  0.0 100.1 jit_solution(2538967461487775858)
XLA Ops:
  7.2 0.0 copy-start
  7.2 0.7 iota_compare_fusion
  7.9 0.7 iota_compare_fusion.1
  8.6 6.4 %all_gather.3 = bf16[16,2048]{1,0:T(8,128)(2,1)S(1)} all-gather(bf16[16,512]{1,0:T(8,128)(2,1)} %param.36), channel_id=1, replica_groups=mesh['parts'=2,'expert'=4,'tensor'=4] {'tensor'}, dimensions={1}, use_global_device_ids=true | all-gather | bytes 81920 | tf_op jit(solution)/shard_map/all_gather | solution.py:135
  15.1 0.9 convolution_convert_fusion
  16.0 5.3 %all-to-all-start = ((bf16[4,2,8,2048]{3,2,1,0:T(8,128)(2,1)}), bf16[4,2,8,2048]{3,2,1,0:T(8,128)(2,1)S(1)}, u32[]{:S(2)}, u32[]{:S(2)}) async-start(bf16[4,2,8,2048]{3,2,1,0:T(8,128)(2,1)} %bitcast.6), calls=%async_computation | async-start | bytes 524288 | tf_op jit(solution)/shard_map/all_to_all | solution.py:142
  21.3 0.0 reduce-scatter.2.cloned.1.call-start
  21.3 0.7 iota_compare_fusion.2
  22.0 0.7 slice_bitcast_fusion
  22.8 0.9 fusion.42
  23.7 2.0 %fusion.49 = (f32[16,2,4]{2,1,0:T(2,128)S(1)}, f32[16,2,4,128]{3,2,1,0:T(4,128)S(1)}) fusion(bf16[16,2,4,128]{3,2,1,0:T(4,128)(2,1)} %bitcast.69, bf16[16,2,128,256]{3,2,1,0:T(8,128)(2,1)} %param.34, pred[16,128]{1,0:T(8,128)(4,1)S(1)} %iota_compare_fusion.2), kind=kOutput, calls=%fused_computation.64 | convolution fusion | flops 4243328 | bytes 1149440 | tf_op jit(solution)/shard_map/sgqd,sgld->sgql/dot_general | solution.py:60
  25.7 0.2 fusion.37
  26.0 0.9 exp.29
  26.8 1.7 %fusion.24 = bf16[16,2,4,128]{3,2,1,0:T(4,128)(2,1)S(1)} fusion(bf16[16,2,128,256]{3,2,1,0:T(8,128)(2,1)} %param.34, f32[16,2,4,128]{3,2,1,0:T(4,128)S(1)} %get-tuple-element.15, f32[16,2,128]{2,1,0:T(2,128)S(1)} %get-tuple-element.13, f32[16,2,4]{2,1,0:T(2,128)S(1)} %get-tuple-element.9, f32[16,2,4]{2,1,0:T(2,128)S(1)} %get-tuple-element.8, ...), kind=kOutput, calls=%fused_computation.18 | convolution fusion | flops 4292608 | bytes 1164800 | tf_op jit(solution)/shard_map/sgql,sgld->sgqd/dot_general | solution.py:85
  28.5 0.6 convert_element_type.48
  29.1 0.9 multiply_reduce_fusion.1
  30.1 0.6 all-to-all-done
  30.7 8.4 %fusion.11 = f32[4,2,8,2048]{3,2,0,1:T(8,128)S(1)} fusion(bf16[2,2,2048,2048]{3,2,1,0:T(8,128)(2,1)} %param.40, bf16[4,2,8,2048]{3,2,1,0:T(8,128)(2,1)S(1)} %all-to-all-done), kind=kOutput, calls=%fused_computation.9 | convolution fusion | flops 536870912 | bytes 17563648 | tf_op jit(solution)/shard_map/nlcd,lfd->nlcf/dot_general | solution.py:143
  39.1 8.7 %fusion.20 = bf16[4,2,8,2048]{3,2,0,1:T(8,128)(2,1)S(1)} fusion(bf16[2,2,2048,2048]{3,2,1,0:T(8,128)(2,1)} %param.40, f32[4,2,8,2048]{3,2,0,1:T(8,128)S(1)} %fusion.11, bf16[4,2,8,2048]{3,2,1,0:T(8,128)(2,1)S(1)} %all-to-all-done), kind=kOutput, calls=%fused_computation.13 | convolution fusion | flops 537657344 | bytes 17825792 | tf_op jit(solution)/shard_map/nlcd,lfd->nlcf/dot_general | solution.py:144
  47.8 0.0 copy-start.3
  47.8 0.0 copy-start.5
  47.8 0.0 copy-start.6
  47.8 0.0 copy-start.7
  47.9 0.0 copy-start.1
  47.9 0.0 copy-start.2
  47.9 0.0 copy-start.4
  47.9 9.5 %fusion.8 = f32[4,2,8,2048]{3,2,0,1:T(8,128)} fusion(bf16[4,2,8,2048]{3,2,0,1:T(8,128)(2,1)S(1)} %fusion.20, bf16[2,2048,2048]{2,1,0:T(8,128)(2,1)} %param.41), kind=kOutput, calls=%fused_computation.8 | convolution fusion | flops 536870912 | bytes 17563648 | tf_op jit(solution)/shard_map/nlcf,lfd->nlcd/dot_general | solution.py:146
  57.4 0.0 reduce-scatter.2.cloned.1.call-update
  57.5 0.0 copy-done
  57.5 0.0 copy-done.3
  57.5 0.3 fusion.40
  57.7 10.7 %psum.7 = f32[16,288]{1,0:T(8,128)S(1)} all-reduce(f32[16,288]{1,0:T(8,128)S(1)} %fusion.40), channel_id=1, replica_groups=mesh['parts'=2,'expert'=4,'tensor'=4] {'tensor'}, use_global_device_ids=true, to_apply=%region_1.2 | all-reduce | flops 4608 | bytes 36864 | tf_op jit(solution)/shard_map/psum | solution.py:32
  68.4 0.0 copy-done.5
  68.5 0.1 fusion.48
  68.6 0.0 copy-done.6
  68.6 0.0 copy-done.7
  68.6 0.2 fusion.47
  68.8 0.0 copy-done.1
  68.8 1.5 %multiply_reduce_fusion = (f32[16,1024]{1,0:T(8,128)S(1)}, f32[16,16,1024]{2,1,0:T(8,128)}) fusion(f32[16,16]{1,0:T(8,128)S(1)} %get-tuple-element.11, f32[16,16]{1,0:T(8,128)S(1)} %get-tuple-element.10, f32[16,1024]{1,0:T(8,128)S(1)} %get-tuple-element.7, f32[16,16,1024]{2,1,0:T(8,128)S(1)} %copy-done.1, f32[16,1024]{1,0:T(8,128)S(1)} %exp.29, ...), kind=kLoop, calls=%fused_computation.23 | loop fusion | flops 1556480 | bytes 2361344 | tf_op jit(solution)/shard_map/reduce_sum | solution.py:45
  70.3 9.9 %reduce-scatter.2.cloned.1.call-done = f32[4,2,8,512]{3,2,0,1:T(8,128)} async-done(((f32[4,2,8,2048]{3,2,0,1:T(8,128)}), f32[4,2,8,512]{3,2,0,1:T(8,128)}) %reduce-scatter.2.cloned.1.call-update) | async-done | bytes 131088 | tf_op jit(solution)/shard_map/reduce_scatter | solution.py:149
  80.2 1.5 %copy.50 = f32[4,2,8,512]{3,2,1,0:T(8,128)} copy(f32[4,2,8,512]{3,2,0,1:T(8,128)} %reduce-scatter.2.cloned.1.call-done) | data formatting | bytes 262144 | tf_op jit(solution)/shard_map/reduce_scatter | solution.py:149
  81.7 4.6 %all-to-all-start.1 = ((f32[4,2,8,512]{3,2,1,0:T(8,128)}), f32[4,2,8,512]{3,2,1,0:T(8,128)S(1)}, u32[]{:S(2)}, u32[]{:S(2)}) async-start(f32[4,2,8,512]{3,2,1,0:T(8,128)} %copy.50), calls=%async_computation.2 | async-start | bytes 262144 | tf_op jit(solution)/shard_map/all_to_all | solution.py:150
  86.3 0.0 copy-done.2
  86.3 0.0 copy-done.4
  86.3 0.7 fusion.36
  87.0 5.4 %all-to-all-done.1 = f32[4,2,8,512]{3,2,1,0:T(8,128)S(1)} async-done(((f32[4,2,8,512]{3,2,1,0:T(8,128)}), f32[4,2,8,512]{3,2,1,0:T(8,128)S(1)}, u32[]{:S(2)}, u32[]{:S(2)}) %all-to-all-start.1) | async-done | bytes 131104 | tf_op jit(solution)/shard_map/all_to_all | solution.py:150
  92.4 0.8 fusion.25
  (4 shorter events, 0.1 us)
Async XLA Ops:
  7.2 50.3 %copy-start = (bf16[288,1024]{1,0:T(8,128)(2,1)S(1)}, bf16[288,1024]{1,0:T(8,128)(2,1)}, u32[]{:S(2)}) copy-start(bf16[288,1024]{1,0:T(8,128)(2,1)} %param.27) | copy-start | bytes 1769476
  16.0 14.7 %all-to-all-start = ((bf16[4,2,8,2048]{3,2,1,0:T(8,128)(2,1)}), bf16[4,2,8,2048]{3,2,1,0:T(8,128)(2,1)S(1)}, u32[]{:S(2)}, u32[]{:S(2)}) async-start(bf16[4,2,8,2048]{3,2,1,0:T(8,128)(2,1)} %bitcast.6), calls=%async_computation | async-start | bytes 524288 | tf_op jit(solution)/shard_map/all_to_all | solution.py:142
  21.3 58.9 %reduce-scatter.2.cloned.1.call-start = ((), (), s32[]{:S(2)}) async-start(), calls=%async_computation.3 | async-start | bytes 655360 | tf_op jit(solution)/shard_map/reduce_scatter | solution.py:149
  47.8 9.7 %copy-start.3 = (f32[1024]{0:T(1024)S(1)}, f32[1024]{0:T(1024)}, u32[]{:S(2)}) copy-start(f32[1024]{0:T(1024)} %param.26) | copy-start | bytes 12292
  47.8 20.6 %copy-start.5 = (f32[16,2]{0,1:T(2,128)S(1)}, f32[16,2]{0,1:T(2,128)}, u32[]{:S(2)}) copy-start(f32[16,2]{0,1:T(2,128)} %param.39) | copy-start | bytes 388
  47.8 20.7 %copy-start.6 = (bf16[256,1024]{1,0:T(8,128)(2,1)S(1)}, bf16[256,1024]{1,0:T(8,128)(2,1)}, u32[]{:S(2)}) copy-start(bf16[256,1024]{1,0:T(8,128)(2,1)} %param.28) | copy-start | bytes 1572868
  47.8 20.7 %copy-start.7 = (f32[1024]{0:T(1024)S(1)}, f32[1024]{0:T(1024)}, u32[]{:S(2)}) copy-start(f32[1024]{0:T(1024)} %param.29) | copy-start | bytes 12292
  47.9 20.9 %copy-start.1 = (f32[16,16,1024]{2,1,0:T(8,128)S(1)}, f32[16,16,1024]{2,1,0:T(8,128)}, u32[]{:S(2)}) copy-start(f32[16,16,1024]{2,1,0:T(8,128)} %param.24) | copy-start | bytes 3145732
  47.9 38.5 %copy-start.2 = (bf16[16,1024]{1,0:T(8,128)(2,1)S(1)}, bf16[16,1024]{1,0:T(8,128)(2,1)}, u32[]{:S(2)}) copy-start(bf16[16,1024]{1,0:T(8,128)(2,1)} %param.22) | copy-start | bytes 98308
  47.9 38.5 %copy-start.4 = (f32[1024]{0:T(1024)S(1)}, f32[1024]{0:T(1024)}, u32[]{:S(2)}) copy-start(f32[1024]{0:T(1024)} %param.31) | copy-start | bytes 12292
  81.7 10.7 %all-to-all-start.1 = ((f32[4,2,8,512]{3,2,1,0:T(8,128)}), f32[4,2,8,512]{3,2,1,0:T(8,128)S(1)}, u32[]{:S(2)}, u32[]{:S(2)}) async-start(f32[4,2,8,512]{3,2,1,0:T(8,128)} %copy.50), calls=%async_computation.2 | async-start | bytes 262144 | tf_op jit(solution)/shard_map/all_to_all | solution.py:150
Sparse Core Ops, SparseCore 0:
  57.6 22.5 reduce-scatter.1
where the time goes:
time: 101 us; the launch traced here: 100 us
  matrix products  33.4 us (33%)
  blocking collectives  17.1 us (17%)
  waiting for transfers between devices  16 us (16%)
  between operations  14.2 us (14%)
  starting transfers between devices  9.95 us (10%)
  other arithmetic  6.26 us (6%)
  local copies, waits for them, and re-layouts  3.17 us (3%)
    psum x1, blocking collectives, mamba_step(): mixing = lax.psum(local_mix, 'tensor')  10.7 us
    reduce_scatter x1, waiting for transfers between devices, shards(): lax.psum_scatter(partial_value, 'tensor', scatter_dimension=3, tiled=True)  9.91 us
    dot_general x1, matrix products, shards(): jnp.einsum('nlcf,lfd->nlcd', hidden, outer_weights, preferred_element_typ...  9.55 us
    dot_general x1, matrix products, shards(): jnp.einsum('nlcd,lfd->nlcf', received, up_rows, preferred_element_type=jn...  8.68 us
    dot_general x1, matrix products, shards(): jnp.einsum('nlcd,lfd->nlcf', received, gate_rows, preferred_element_type=...  8.42 us
    all_gather x1, blocking collectives, shards(): features = lax.all_gather(expert_input, 'tensor', axis=1, tiled=True)  6.44 us
    all_to_all x1, waiting for transfers between devices, shards(): lax.all_to_all(share_sum, 'expert', split_axis=0, concat_axis=0, tiled=True)  5.4 us
    all_to_all x1, starting transfers between devices, shards(): lax.all_to_all(outgoing, 'expert', split_axis=0, concat_axis=0, tiled=True)  5.34 us
  transfers between devices with their start and end apart: 3, of which 3 were waited for; matrix products, arithmetic and copies ran while one was open for 11% of the time, Pallas kernels for 0%

commit v1 on v0

--- a/solution.py
+++ b/solution.py
@@ -2,6 +2,7 @@
 import jax.numpy as jnp
 from jax import lax
 from jax.sharding import PartitionSpec as P
+from jax.lax import axis_size, ppermute
 
 EXPERTS = 8
 
@@ -29,7 +30,11 @@
         (((1,), (1,)), ((), ())),
         preferred_element_type=jnp.float32,
     )
-    mixing = lax.psum(local_mix, "tensor")
+    n_parts = axis_size("tensor")
+    mixing = local_mix
+    for at in [[(jj, jj ^ h) for jj in range(n_parts)] for h in (1, 2, 4, 8, 16) if h < n_parts]:
+        state_now = ppermute(mixing, axis_name="tensor", perm=at)
+        mixing = mixing + state_now
     low_rank = step_proj.shape[0]
     states = decay_log.shape[0]
     step_size = jax.nn.softplus(

time: 101 us -> 101 us (level)
  blocking collectives: 17.1 us -> 6.37 us
  waiting for transfers between devices: 16 us -> 25.4 us
  starting transfers between devices: 9.95 us -> 11.6 us
    psum x1 -> x0, blocking collectives: 10.7 us -> none  [mamba_step(): mixing = lax.psum(local_mix, 'tensor')]
    all_to_all x1, waiting for transfers between devices: 0.62 us -> 4.73 us  [shards(): lax.all_to_all(outgoing, 'expert', split_axis=0, concat_axis=0, tiled=True)]
    reduce_scatter x1, waiting for transfers between devices: 9.91 us -> 13.6 us  [shards(): lax.psum_scatter(partial_value, 'tensor', scatter_dimension=3, tiled=True)]
    ppermute x0 -> x2, starting transfers between devices: none -> 2.07 us  [mamba_step(): state_now = ppermute(mixing, axis_name='tensor', perm=at)]
    ppermute x0 -> x2, waiting for transfers between devices: none -> 1.65 us  [mamba_step(): state_now = ppermute(mixing, axis_name='tensor', perm=at)]
  transfers between devices with their start and end apart: 3 -> 5, of which waited for: 3 -> 4; matrix products, arithmetic and copies ran while one was open for 11% -> 38% of each run, Pallas kernels for 0% -> 0%
where the time goes in v1:
time: 101 us; the launch traced here: 100 us
  matrix products  34.1 us (34%)
  waiting for transfers between devices  25.4 us (25%)
  between operations  14.2 us (14%)
  starting transfers between devices  11.6 us (11%)
  blocking collectives  6.37 us (6%)
  other arithmetic  6.26 us (6%)
  local copies, waits for them, and re-layouts  2.48 us (2%)
    reduce_scatter x1, waiting for transfers between devices, shards(): lax.psum_scatter(partial_value, 'tensor', scatter_dimension=3, tiled=True)  13.6 us
    dot_general x1, matrix products, shards(): jnp.einsum('nlcf,lfd->nlcd', hidden, outer_weights, preferred_element_typ...  9.54 us
    dot_general x1, matrix products, shards(): jnp.einsum('nlcd,lfd->nlcf', received, up_rows, preferred_element_type=jn...  8.67 us
    dot_general x1, matrix products, shards(): jnp.einsum('nlcd,lfd->nlcf', received, gate_rows, preferred_element_type=...  8.42 us
    all_gather x1, blocking collectives, shards(): features = lax.all_gather(expert_input, 'tensor', axis=1, tiled=True)  6.37 us
    all_to_all x1, waiting for transfers between devices, shards(): lax.all_to_all(share_sum, 'expert', split_axis=0, concat_axis=0, tiled=True)  5.4 us
    all_to_all x1, starting transfers between devices, shards(): lax.all_to_all(outgoing, 'expert', split_axis=0, concat_axis=0, tiled=True)  4.92 us
    all_to_all x1, waiting for transfers between devices, shards(): lax.all_to_all(outgoing, 'expert', split_axis=0, concat_axis=0, tiled=True)  4.73 us
  transfers between devices with their start and end apart: 5, of which 4 were waited for; matrix products, arithmetic and copies ran while one was open for 38% of the time, Pallas kernels for 0%

profile of v1, /device:TPU:0, one launch (start us, length us, event | category | flops | bytes accessed | tf_op | source)
XLA Modules:
  0.0 100.3 jit_solution(13140190848744721310)
XLA Ops:
  7.2 0.0 copy-start
  7.2 1.0 multiply_reduce_fusion.1
  8.2 0.1 copy-done
  8.3 0.9 fusion.40
  9.3 0.5 collective-permute-start
  9.8 0.7 iota_compare_fusion
  10.5 0.7 iota_compare_fusion.1
  11.1 6.4 %all_gather.3 = bf16[16,2048]{1,0:T(8,128)(2,1)S(1)} all-gather(bf16[16,512]{1,0:T(8,128)(2,1)} %param.36), channel_id=1, replica_groups=mesh['parts'=2,'expert'=4,'tensor'=4] {'tensor'}, dimensions={1}, use_global_device_ids=true | all-gather | bytes 81920 | tf_op jit(solution)/shard_map/all_gather | solution.py:140
  17.5 0.9 convolution_convert_fusion
  18.4 4.9 %all-to-all-start = ((bf16[4,2,8,2048]{3,2,1,0:T(8,128)(2,1)}), bf16[4,2,8,2048]{3,2,1,0:T(8,128)(2,1)S(1)}, u32[]{:S(2)}, u32[]{:S(2)}) async-start(bf16[4,2,8,2048]{3,2,1,0:T(8,128)(2,1)} %bitcast.6), calls=%async_computation | async-start | bytes 524288 | tf_op jit(solution)/shard_map/all_to_all | solution.py:147
  23.4 0.0 reduce-scatter.2.cloned.1.call-start
  23.4 0.7 iota_compare_fusion.2
  24.1 0.7 slice_bitcast_fusion
  24.8 0.9 fusion.42
  25.7 2.0 %fusion.49 = (f32[16,2,4]{2,1,0:T(2,128)S(1)}, f32[16,2,4,128]{3,2,1,0:T(4,128)S(1)}) fusion(bf16[16,2,4,128]{3,2,1,0:T(4,128)(2,1)} %bitcast.69, bf16[16,2,128,256]{3,2,1,0:T(8,128)(2,1)} %param.34, pred[16,128]{1,0:T(8,128)(4,1)S(1)} %iota_compare_fusion.2), kind=kOutput, calls=%fused_computation.64 | convolution fusion | flops 4243328 | bytes 1149440 | tf_op jit(solution)/shard_map/sgqd,sgld->sgql/dot_general | solution.py:65
  27.7 0.2 fusion.37
  28.0 4.7 %all-to-all-done = bf16[4,2,8,2048]{3,2,1,0:T(8,128)(2,1)S(1)} async-done(((bf16[4,2,8,2048]{3,2,1,0:T(8,128)(2,1)}), bf16[4,2,8,2048]{3,2,1,0:T(8,128)(2,1)S(1)}, u32[]{:S(2)}, u32[]{:S(2)}) %all-to-all-start) | async-done | bytes 262176 | tf_op jit(solution)/shard_map/all_to_all | solution.py:147
  32.7 8.4 %fusion.11 = f32[4,2,8,2048]{3,2,0,1:T(8,128)S(1)} fusion(bf16[2,2,2048,2048]{3,2,1,0:T(8,128)(2,1)} %param.40, bf16[4,2,8,2048]{3,2,1,0:T(8,128)(2,1)S(1)} %all-to-all-done), kind=kOutput, calls=%fused_computation.9 | convolution fusion | flops 536870912 | bytes 17563648 | tf_op jit(solution)/shard_map/nlcd,lfd->nlcf/dot_general | solution.py:148
  41.2 8.7 %fusion.20 = bf16[4,2,8,2048]{3,2,0,1:T(8,128)(2,1)S(1)} fusion(bf16[2,2,2048,2048]{3,2,1,0:T(8,128)(2,1)} %param.40, f32[4,2,8,2048]{3,2,0,1:T(8,128)S(1)} %fusion.11, bf16[4,2,8,2048]{3,2,1,0:T(8,128)(2,1)S(1)} %all-to-all-done), kind=kOutput, calls=%fused_computation.13 | convolution fusion | flops 537657344 | bytes 17825792 | tf_op jit(solution)/shard_map/nlcd,lfd->nlcf/dot_general | solution.py:149
  49.8 0.0 copy-start.6
  49.9 0.0 copy-start.2
  49.9 0.0 copy-start.4
  49.9 0.0 copy-start.7
  49.9 0.0 copy-start.8
  49.9 0.0 copy-start.1
  49.9 0.0 copy-start.3
  49.9 0.0 copy-start.5
  49.9 9.5 %fusion.8 = f32[4,2,8,2048]{3,2,0,1:T(8,128)} fusion(bf16[4,2,8,2048]{3,2,0,1:T(8,128)(2,1)S(1)} %fusion.20, bf16[2,2048,2048]{2,1,0:T(8,128)(2,1)} %param.41), kind=kOutput, calls=%fused_computation.8 | convolution fusion | flops 536870912 | bytes 17563648 | tf_op jit(solution)/shard_map/nlcf,lfd->nlcd/dot_general | solution.py:151
  59.5 0.0 reduce-scatter.2.cloned.1.call-update
  59.5 1.7 %fusion.24 = bf16[16,2,4,128]{3,2,1,0:T(4,128)(2,1)S(1)} fusion(bf16[16,2,128,256]{3,2,1,0:T(8,128)(2,1)} %param.34, f32[16,2,4,128]{3,2,1,0:T(4,128)S(1)} %get-tuple-element.15, f32[16,2,128]{2,1,0:T(2,128)S(1)} %get-tuple-element.13, f32[16,2,4]{2,1,0:T(2,128)S(1)} %get-tuple-element.9, f32[16,2,4]{2,1,0:T(2,128)S(1)} %get-tuple-element.8, ...), kind=kOutput, calls=%fused_computation.18 | convolution fusion | flops 4292608 | bytes 1164800 | tf_op jit(solution)/shard_map/sgql,sgld->sgqd/dot_general | solution.py:90
  61.2 0.0 collective-permute-done
  61.2 1.6 %collective-permute-start.1 = (f32[16,288]{1,0:T(8,128)S(1)}, f32[16,288]{1,0:T(8,128)S(1)}, u32[]{:S(2)}, u32[]{:S(2)}) collective-permute-start(f32[16,288]{1,0:T(8,128)S(1)} %add.56), channel_id=1, source_target_pairs={{0,2},{1,3},{2,0},{3,1},{4,6},{5,7},{6,4},{7,5},{8,10},{9,11},{10,... | collective-permute-start | bytes 55304 | tf_op jit(solution)/shard_map/ppermute | solution.py:36
  62.8 0.0 copy-done.6
  62.8 0.0 copy-done.2
  62.8 0.6 convert_element_type.48
  63.4 1.6 %collective-permute-done.1 = f32[16,288]{1,0:T(8,128)S(1)} collective-permute-done((f32[16,288]{1,0:T(8,128)S(1)}, f32[16,288]{1,0:T(8,128)S(1)}, u32[]{:S(2)}, u32[]{:S(2)}) %collective-permute-start.1) | collective-permute-done | bytes 18464 | tf_op jit(solution)/shard_map/ppermute | solution.py:36
  65.1 0.1 fusion.48
  65.2 0.0 copy-done.4
  65.2 0.0 copy-done.7
  65.2 0.0 copy-done.8
  65.2 0.2 fusion.47
  65.4 0.0 copy-done.1
  65.4 1.5 %multiply_reduce_fusion = (f32[16,1024]{1,0:T(8,128)S(1)}, f32[16,16,1024]{2,1,0:T(8,128)}) fusion(f32[16,16]{1,0:T(8,128)S(1)} %get-tuple-element.11, f32[16,16]{1,0:T(8,128)S(1)} %get-tuple-element.10, f32[16,1024]{1,0:T(8,128)S(1)} %get-tuple-element.7, f32[16,16,1024]{2,1,0:T(8,128)S(1)} %copy-done.1, f32[16,1024]{1,0:T(8,128)S(1)} %exp.29, ...), kind=kLoop, calls=%fused_computation.23 | loop fusion | flops 1556480 | bytes 2361344 | tf_op jit(solution)/shard_map/reduce_sum | solution.py:50
  66.9 13.6 %reduce-scatter.2.cloned.1.call-done = f32[4,2,8,512]{3,2,0,1:T(8,128)} async-done(((f32[4,2,8,2048]{3,2,0,1:T(8,128)}), f32[4,2,8,512]{3,2,0,1:T(8,128)}) %reduce-scatter.2.cloned.1.call-update) | async-done | bytes 131088 | tf_op jit(solution)/shard_map/reduce_scatter | solution.py:154
  80.4 1.6 %copy.50 = f32[4,2,8,512]{3,2,1,0:T(8,128)} copy(f32[4,2,8,512]{3,2,0,1:T(8,128)} %reduce-scatter.2.cloned.1.call-done) | data formatting | bytes 262144 | tf_op jit(solution)/shard_map/reduce_scatter | solution.py:154
  82.0 4.6 %all-to-all-start.1 = ((f32[4,2,8,512]{3,2,1,0:T(8,128)}), f32[4,2,8,512]{3,2,1,0:T(8,128)S(1)}, u32[]{:S(2)}, u32[]{:S(2)}) async-start(f32[4,2,8,512]{3,2,1,0:T(8,128)} %copy.50), calls=%async_computation.2 | async-start | bytes 262144 | tf_op jit(solution)/shard_map/all_to_all | solution.py:155
  86.6 0.0 copy-done.3
  86.6 0.0 copy-done.5
  86.6 0.7 fusion.36
  87.3 5.4 %all-to-all-done.1 = f32[4,2,8,512]{3,2,1,0:T(8,128)S(1)} async-done(((f32[4,2,8,512]{3,2,1,0:T(8,128)}), f32[4,2,8,512]{3,2,1,0:T(8,128)S(1)}, u32[]{:S(2)}, u32[]{:S(2)}) %all-to-all-start.1) | async-done | bytes 131104 | tf_op jit(solution)/shard_map/all_to_all | solution.py:155
  92.7 0.8 fusion.25
  (7 shorter events, 0.1 us)
Async XLA Ops:
  7.2 1.1 %copy-start = (bf16[288,1024]{1,0:T(8,128)(2,1)S(1)}, bf16[288,1024]{1,0:T(8,128)(2,1)}, u32[]{:S(2)}) copy-start(bf16[288,1024]{1,0:T(8,128)(2,1)} %param.27) | copy-start | bytes 1769476
  9.3 51.9 %collective-permute-start = (f32[16,288]{1,0:T(8,128)S(1)}, f32[16,288]{1,0:T(8,128)S(1)}, u32[]{:S(2)}, u32[]{:S(2)}) collective-permute-start(f32[16,288]{1,0:T(8,128)S(1)} %fusion.40), channel_id=1, source_target_pairs={{0,1},{1,0},{2,3},{3,2},{4,5},{5,4},{6,7},{7,6},{8,9},{9,8},{10,11... | collective-permute-start | bytes 55304 | tf_op jit(solution)/shard_map/ppermute | solution.py:36
  18.4 14.3 %all-to-all-start = ((bf16[4,2,8,2048]{3,2,1,0:T(8,128)(2,1)}), bf16[4,2,8,2048]{3,2,1,0:T(8,128)(2,1)S(1)}, u32[]{:S(2)}, u32[]{:S(2)}) async-start(bf16[4,2,8,2048]{3,2,1,0:T(8,128)(2,1)} %bitcast.6), calls=%async_computation | async-start | bytes 524288 | tf_op jit(solution)/shard_map/all_to_all | solution.py:147
  23.4 57.1 %reduce-scatter.2.cloned.1.call-start = ((), (), s32[]{:S(2)}) async-start(), calls=%async_computation.3 | async-start | bytes 655360 | tf_op jit(solution)/shard_map/reduce_scatter | solution.py:154
  49.8 12.9 %copy-start.6 = (f32[16,2]{0,1:T(2,128)S(1)}, f32[16,2]{0,1:T(2,128)}, u32[]{:S(2)}) copy-start(f32[16,2]{0,1:T(2,128)} %param.39) | copy-start | bytes 388
  49.9 12.9 %copy-start.2 = (f32[16,1024]{1,0:T(8,128)S(1)}, f32[16,1024]{1,0:T(8,128)}, u32[]{:S(2)}) copy-start(f32[16,1024]{1,0:T(8,128)} %param.30) | copy-start | bytes 196612
  49.9 15.3 %copy-start.4 = (f32[1024]{0:T(1024)S(1)}, f32[1024]{0:T(1024)}, u32[]{:S(2)}) copy-start(f32[1024]{0:T(1024)} %param.26) | copy-start | bytes 12292
  49.9 15.3 %copy-start.7 = (bf16[256,1024]{1,0:T(8,128)(2,1)S(1)}, bf16[256,1024]{1,0:T(8,128)(2,1)}, u32[]{:S(2)}) copy-start(bf16[256,1024]{1,0:T(8,128)(2,1)} %param.28) | copy-start | bytes 1572868
  49.9 15.3 %copy-start.8 = (f32[1024]{0:T(1024)S(1)}, f32[1024]{0:T(1024)}, u32[]{:S(2)}) copy-start(f32[1024]{0:T(1024)} %param.29) | copy-start | bytes 12292
  49.9 15.5 %copy-start.1 = (f32[16,16,1024]{2,1,0:T(8,128)S(1)}, f32[16,16,1024]{2,1,0:T(8,128)}, u32[]{:S(2)}) copy-start(f32[16,16,1024]{2,1,0:T(8,128)} %param.24) | copy-start | bytes 3145732
  49.9 36.7 %copy-start.3 = (bf16[16,1024]{1,0:T(8,128)(2,1)S(1)}, bf16[16,1024]{1,0:T(8,128)(2,1)}, u32[]{:S(2)}) copy-start(bf16[16,1024]{1,0:T(8,128)(2,1)} %param.22) | copy-start | bytes 98308
  49.9 36.7 %copy-start.5 = (f32[1024]{0:T(1024)S(1)}, f32[1024]{0:T(1024)}, u32[]{:S(2)}) copy-start(f32[1024]{0:T(1024)} %param.31) | copy-start | bytes 12292
  61.2 3.9 %collective-permute-start.1 = (f32[16,288]{1,0:T(8,128)S(1)}, f32[16,288]{1,0:T(8,128)S(1)}, u32[]{:S(2)}, u32[]{:S(2)}) collective-permute-start(f32[16,288]{1,0:T(8,128)S(1)} %add.56), channel_id=1, source_target_pairs={{0,2},{1,3},{2,0},{3,1},{4,6},{5,7},{6,4},{7,5},{8,10},{9,11},{10,... | collective-permute-start | bytes 55304 | tf_op jit(solution)/shard_map/ppermute | solution.py:36
  82.0 10.6 %all-to-all-start.1 = ((f32[4,2,8,512]{3,2,1,0:T(8,128)}), f32[4,2,8,512]{3,2,1,0:T(8,128)S(1)}, u32[]{:S(2)}, u32[]{:S(2)}) async-start(f32[4,2,8,512]{3,2,1,0:T(8,128)} %copy.50), calls=%async_computation.2 | async-start | bytes 262144 | tf_op jit(solution)/shard_map/all_to_all | solution.py:155
Sparse Core Ops, SparseCore 0:
  59.6 20.7 reduce-scatter.1
